TPU v7x, 32 devices: a whole 2x2x4 slice. The times are simulated.
32 devices in a mesh: row: 2 (over y), col: 16 (over z, x, core).
Axes of the slice: x: 2, y: 2, z: 4, core: 2. Of those that a mesh axis runs over, the one named last changes fastest.
Arguments:
- image_student: bfloat16 [2048, 1024], P(('row', 'col')), may hold values from -2.5 to 2.5
- text_student: bfloat16 [2048, 1024], P(('col', 'row')), may hold values from -2.5 to 2.5
- image_teacher: bfloat16 [2048, 1024], P(('row', 'col')), may hold values from -2.5 to 2.5
- text_teacher: bfloat16 [2048, 1024], P(('col', 'row')), may hold values from -2.5 to 2.5
Outputs:
- loss: float32 [], replicated
- image_grad: float32 [2048, 1024], P(('row', 'col'))
- text_grad: float32 [2048, 1024], P(('col', 'row'))
All inputs are finite; a program needn't handle non-finite values.
Results may differ from a plain program's by a relative error of at most 0.002.
Values may be sent and summed in bfloat16 or wider, within the bound.
A program may use at most 128 MiB of HBM per device.

v0:
```python
import jax
import jax.numpy as jnp
from jax import lax
from jax.sharding import PartitionSpec as P

logit_scale = 100.0


def joined(value, axis, join):
    pieces = jax.tree.map(lambda part: lax.all_gather(part, axis), value)
    head = jax.tree.map(lambda part: part[0], pieces)
    tail = jax.tree.map(lambda part: part[1:], pieces)
    subtotal, _ = lax.scan(lambda subtotal, slab: (join(subtotal, slab), None), head, tail)
    return subtotal


def tile_logits(left, right):
    return logit_scale * lax.dot_general(
        left, right, (((1,), (1,)), ((), ())), preferred_element_type=jnp.float32
    )


def partial_stats(student, teacher, along):
    student_high = jnp.max(student, along, keepdims=True)
    student_total = jnp.sum(jnp.exp(student - student_high), along)
    teacher_high = jnp.max(teacher, along, keepdims=True)
    weights = jnp.exp(teacher - teacher_high)
    teacher_total = jnp.sum(weights, along)
    divergence = jnp.sum(weights * (teacher - student), along)
    return (
        jnp.squeeze(student_high, along),
        student_total,
        jnp.squeeze(teacher_high, along),
        teacher_total,
        divergence,
    )


def merge_stats(first, second):
    student_high = jnp.maximum(first[0], second[0])
    teacher_high = jnp.maximum(first[2], second[2])
    early = jnp.exp(first[2] - teacher_high)
    later = jnp.exp(second[2] - teacher_high)
    student_total = first[1] * jnp.exp(first[0] - student_high) + second[1] * jnp.exp(
        second[0] - student_high
    )
    return (
        student_high,
        student_total,
        teacher_high,
        first[3] * early + second[3] * later,
        first[4] * early + second[4] * later,
    )


def finish(stats):
    student_lse = stats[0] + jnp.log(stats[1])
    teacher_lse = stats[2] + jnp.log(stats[3])
    divergence = stats[4] / stats[3] - teacher_lse + student_lse
    return (student_lse, teacher_lse, 0.5 * (student_lse + divergence))


def body(image_student, text_student, image_teacher, text_teacher):
    per_device = image_student.shape[0]
    image_slab, image_frozen = (
        lax.all_gather(image_student, "col", axis=0, tiled=True),
        lax.all_gather(image_teacher, "col", axis=0, tiled=True),
    )
    text_slab, text_frozen = (
        lax.all_gather(text_student, "row", axis=0, tiled=True),
        lax.all_gather(text_teacher, "row", axis=0, tiled=True),
    )
    student = tile_logits(image_slab, text_slab)
    teacher = tile_logits(image_frozen, text_frozen)
    row_stats = joined(partial_stats(student, teacher, 1), "col", merge_stats)
    column_stats = joined(partial_stats(student, teacher, 0), "row", merge_stats)
    student_rows, teacher_rows, row_terms = finish(row_stats)
    student_columns, teacher_columns, column_terms = finish(column_stats)
    row_place = lax.axis_index("row")
    col_place = lax.axis_index("col")
    row_index = row_place * student.shape[0] + jnp.arange(student.shape[0], dtype=jnp.int32)
    column_index = col_place * student.shape[1] + jnp.arange(student.shape[1], dtype=jnp.int32)
    identity = (row_index[:, None] == column_index[None, :]).astype(jnp.float32)
    own_rows = lax.dynamic_slice_in_dim(row_terms, col_place * per_device, per_device)
    own_columns = lax.dynamic_slice_in_dim(column_terms, row_place * per_device, per_device)
    partial_value = jnp.sum(own_rows) + jnp.sum(own_columns) - jnp.sum(student * identity)
    pair_count = per_device * lax.axis_size("row") * lax.axis_size("col")
    loss = lax.psum(partial_value, ("row", "col")) / pair_count
    gradient = (
        jnp.exp(student - student_rows[:, None])
        + jnp.exp(student - student_columns[None, :])
        - 0.5
        * (jnp.exp(teacher - teacher_rows[:, None]) + jnp.exp(teacher - teacher_columns[None, :]))
        - identity
    ).astype(jnp.bfloat16)
    picked = gradient
    image_grad = lax.psum_scatter(
        logit_scale * jnp.dot(picked, text_slab, preferred_element_type=jnp.float32),
        "col",
        scatter_dimension=0,
        tiled=True,
    )
    picked = gradient
    text_grad = lax.psum_scatter(
        logit_scale
        * lax.dot_general(
            picked, image_slab, (((0,), (0,)), ((), ())), preferred_element_type=jnp.float32
        ),
        "row",
        scatter_dimension=0,
        tiled=True,
    )
    return (loss, image_grad, text_grad)


def solution(mesh):
    return jax.shard_map(
        body,
        mesh=mesh,
        in_specs=(
            P(("row", "col"), None),
            P(("col", "row"), None),
            P(("row", "col"), None),
            P(("col", "row"), None),
        ),
        out_specs=(P(), P(("row", "col"), None), P(("col", "row"), None)),
        check_vma=False,
    )
```

profile of v0, /device:TPU:0, one launch (start us, length us, event | category | flops | bytes accessed | tf_op | source)
XLA Modules:
  0.0 348.5 jit_solution(8966833049292975787)
XLA Ops:
  8.7 7.4 %all_gather.61 = bf16[128,1024]{1,0:T(8,128)(2,1)S(1)} all-gather(bf16[64,1024]{1,0:T(8,128)(2,1)} %param.7), channel_id=1, replica_groups=mesh['row'=2,'col'=16] {'row'}, dimensions={0}, use_global_device_ids=true | all-gather | bytes 393216 | tf_op jit(solution)/shard_map/all_gather | solution.py:70
  16.1 5.8 %all_gather.66 = bf16[128,1024]{1,0:T(8,128)(2,1)S(1)} all-gather(bf16[64,1024]{1,0:T(8,128)(2,1)} %param.9), channel_id=1, replica_groups=mesh['row'=2,'col'=16] {'row'}, dimensions={0}, use_global_device_ids=true | all-gather | bytes 393216 | tf_op jit(solution)/shard_map/all_gather | solution.py:71
  22.5 31.8 %all-gather.20.cloned.1.call-done = bf16[1024,1024]{1,0:T(8,128)(2,1)} async-done(((bf16[64,1024]{1,0:T(8,128)(2,1)}), bf16[1024,1024]{1,0:T(8,128)(2,1)}) %all-gather.20.cloned.1.call-update) | async-done | bytes 2097168 | tf_op jit(solution)/shard_map/all_gather | solution.py:67
  54.3 2.9 fusion.37
  57.2 19.3 %all-gather.2 = f32[16384]{0:T(1024)S(1)} all-gather(f32[1024]{0:T(1024)S(1)} %get-tuple-element.112), channel_id=4, replica_groups=mesh['row'=2,'col'=16] {'col'}, dimensions={0}, use_global_device_ids=true | all-gather | bytes 69632 | tf_op jit(solution)/shard_map/all_gather | solution.py:10
  76.5 20.5 %all-gather.18.cloned.1.call-done = bf16[1024,1024]{1,0:T(8,128)(2,1)} async-done(((bf16[64,1024]{1,0:T(8,128)(2,1)}), bf16[1024,1024]{1,0:T(8,128)(2,1)}) %all-gather.18.cloned.1.call-update) | async-done | bytes 2097168 | tf_op jit(solution)/shard_map/all_gather | solution.py:66
  97.0 2.4 fusion.36
  99.4 19.4 %all-gather = f32[16384]{0:T(1024)S(1)} all-gather(f32[1024]{0:T(1024)S(1)} %get-tuple-element.110), channel_id=2, replica_groups=mesh['row'=2,'col'=16] {'col'}, dimensions={0}, use_global_device_ids=true | all-gather | bytes 69632 | tf_op jit(solution)/shard_map/all_gather | solution.py:10
  118.8 2.5 multiply_reduce_fusion
  121.4 17.6 %all-gather.4 = f32[16384]{0:T(1024)S(1)} all-gather(f32[1024]{0:T(1024)S(1)} %get-tuple-element.103), channel_id=6, replica_groups=mesh['row'=2,'col'=16] {'col'}, dimensions={0}, use_global_device_ids=true | all-gather | bytes 69632 | tf_op jit(solution)/shard_map/all_gather | solution.py:10
  139.6 18.9 %all-gather.3 = f32[16384]{0:T(1024)S(1)} all-gather(f32[1024]{0:T(1024)S(1)} %get-tuple-element.104), channel_id=5, replica_groups=mesh['row'=2,'col'=16] {'col'}, dimensions={0}, use_global_device_ids=true | all-gather | bytes 69632 | tf_op jit(solution)/shard_map/all_gather | solution.py:10
  159.1 17.6 %all-gather.1 = f32[16384]{0:T(1024)S(1)} all-gather(f32[1024]{0:T(1024)S(1)} %get-tuple-element.108), channel_id=3, replica_groups=mesh['row'=2,'col'=16] {'col'}, dimensions={0}, use_global_device_ids=true | all-gather | bytes 69632 | tf_op jit(solution)/shard_map/all_gather | solution.py:10
  177.4 4.2 %all-gather.13 = f32[2,1,128]{2,1,0:T(1,128)} all-gather(f32[1,1,128]{2,1,0:T(1,128)S(1)} %bitcast.195), channel_id=10, replica_groups=mesh['row'=2,'col'=16] {'row'}, dimensions={0}, use_global_device_ids=true | all-gather | bytes 1536 | tf_op jit(solution)/shard_map/all_gather | solution.py:10
  182.2 4.4 %all-gather.10 = f32[2,1,128]{2,1,0:T(1,128)S(1)} all-gather(f32[1,1,128]{2,1,0:T(1,128)} %bitcast.196), channel_id=7, replica_groups=mesh['row'=2,'col'=16] {'row'}, dimensions={0}, use_global_device_ids=true | all-gather | bytes 1536 | tf_op jit(solution)/shard_map/all_gather | solution.py:10
  186.6 4.4 %all-gather.14 = f32[2,1,128]{2,1,0:T(1,128)S(1)} all-gather(f32[1,1,128]{2,1,0:T(1,128)} %bitcast.199), channel_id=11, replica_groups=mesh['row'=2,'col'=16] {'row'}, dimensions={0}, use_global_device_ids=true | all-gather | bytes 1536 | tf_op jit(solution)/shard_map/all_gather | solution.py:10
  191.0 4.3 %all-gather.11 = f32[2,1,128]{2,1,0:T(1,128)S(1)} all-gather(f32[1,1,128]{2,1,0:T(1,128)} %bitcast.198), channel_id=8, replica_groups=mesh['row'=2,'col'=16] {'row'}, dimensions={0}, use_global_device_ids=true | all-gather | bytes 1536 | tf_op jit(solution)/shard_map/all_gather | solution.py:10
  195.9 0.8 reshape.44
  196.7 1.5 reshape.43
  198.2 1.5 reshape.41
  199.7 47.1 %while.2 = (s32[]{:T(128)}, f32[1024]{0:T(1024)S(1)}, f32[1024]{0:T(1024)S(1)}, f32[1024]{0:T(1024)S(1)}, f32[1024]{0:T(1024)S(1)}, /*index=5*/f32[1024]{0:T(102...) while((s32[]{:T(128)}, f32[1024]{0:T(1024)S(1)}, ...), condition=%wide.region_6.7_spmd, body=%wide.region_5.6_spmd.sunk | while | flops 17410 | bytes 123025 | solution.py:13
  199.7 0.8 constant_dynamic-slice_fusion.14
  200.5 0.8 constant_dynamic-slice_fusion.11
  201.2 0.8 constant_dynamic-slice_fusion.12
  202.0 0.8 constant_dynamic-slice_fusion.13
  202.8 0.8 constant_dynamic-slice_fusion.14
  203.6 0.8 constant_dynamic-slice_fusion.11
  204.4 0.8 constant_dynamic-slice_fusion.12
  205.1 0.8 constant_dynamic-slice_fusion.13
  206.0 0.8 constant_dynamic-slice_fusion.14
  206.7 0.8 constant_dynamic-slice_fusion.11
  207.5 0.8 constant_dynamic-slice_fusion.12
  208.3 0.8 constant_dynamic-slice_fusion.13
  209.1 0.8 constant_dynamic-slice_fusion.14
  209.9 0.8 constant_dynamic-slice_fusion.11
  210.6 0.8 constant_dynamic-slice_fusion.12
  211.4 0.8 constant_dynamic-slice_fusion.13
  212.3 0.8 constant_dynamic-slice_fusion.14
  213.0 0.8 constant_dynamic-slice_fusion.11
  213.8 0.8 constant_dynamic-slice_fusion.12
  214.6 0.8 constant_dynamic-slice_fusion.13
  215.4 0.8 constant_dynamic-slice_fusion.14
  216.2 0.8 constant_dynamic-slice_fusion.11
  216.9 0.8 constant_dynamic-slice_fusion.12
  217.7 0.8 constant_dynamic-slice_fusion.13
  218.5 0.8 constant_dynamic-slice_fusion.14
  219.3 0.8 constant_dynamic-slice_fusion.11
  220.1 0.8 constant_dynamic-slice_fusion.12
  221.7 0.8 constant_dynamic-slice_fusion.14
  224.8 0.8 constant_dynamic-slice_fusion.14
  225.6 0.8 constant_dynamic-slice_fusion.11
  227.1 0.8 constant_dynamic-slice_fusion.13
  228.0 0.8 constant_dynamic-slice_fusion.14
  231.1 0.8 constant_dynamic-slice_fusion.14
  232.6 0.8 constant_dynamic-slice_fusion.12
  234.2 0.8 constant_dynamic-slice_fusion.14
  237.4 0.8 constant_dynamic-slice_fusion.14
  238.2 0.8 constant_dynamic-slice_fusion.11
  240.5 0.8 constant_dynamic-slice_fusion.14
  243.7 0.8 constant_dynamic-slice_fusion.14
  247.5 2.7 convolution_multiply_fusion.1
  250.3 2.7 convolution_multiply_fusion
  253.6 4.2 %all-gather.12 = f32[2,1,128]{2,1,0:T(1,128)S(1)} all-gather(f32[1,1,128]{2,1,0:T(1,128)S(1)} %bitcast.197), channel_id=9, replica_groups=mesh['row'=2,'col'=16] {'row'}, dimensions={0}, use_global_device_ids=true | all-gather | bytes 1536 | tf_op jit(solution)/shard_map/all_gather | solution.py:10
  261.0 38.3 %psum.7 = f32[]{:T(128)} all-reduce(f32[]{:T(128)S(6)} %sub.142), channel_id=1, replica_groups=mesh['row'=2,'col'=16] {'row','col'}, use_global_device_ids=true, to_apply=%region_15.16 | all-reduce | flops 1 | bytes 8 | tf_op jit(solution)/shard_map/psum | solution.py:88
  300.0 40.8 %reduce-scatter.3.cloned.1.call-done = f32[64,1024]{1,0:T(8,128)} async-done(((f32[1024,1024]{1,0:T(8,128)}), f32[64,1024]{1,0:T(8,128)}) %reduce-scatter.3.cloned.1.call-update) | async-done | bytes 262160 | tf_op jit(solution)/shard_map/reduce_scatter | solution.py:97
  (122 shorter events, 24.6 us)
Async XLA Ops:
  7.2 47.2 %all-gather.20.cloned.1.call-start = ((), (), s32[]{:S(2)}) async-start(), calls=%async_computation.3 | async-start | bytes 2228224 | tf_op jit(solution)/shard_map/all_gather | solution.py:67
  7.9 89.1 %all-gather.18.cloned.1.call-start = ((), (), s32[]{:S(2)}) async-start(), calls=%async_computation.2 | async-start | bytes 2228224 | tf_op jit(solution)/shard_map/all_gather | solution.py:66
  8.6 291.4 %reduce-scatter.5.cloned.1.call-start = ((), (), s32[]{:S(2)}) async-start(), calls=%async_computation.5 | async-start | bytes 786432 | tf_op jit(solution)/shard_map/reduce_scatter | solution.py:104
  97.0 21.9 %copy-start.3 = (f32[128]{0:T(128)S(1)}, f32[128]{0:T(128)}, u32[]{:S(2)}) copy-start(f32[128]{0:T(128)} %get-tuple-element.111) | copy-start | bytes 1540
  99.4 78.0 %copy-start.4 = (f32[128]{0:T(128)}, f32[128]{0:T(128)S(1)}, u32[]{:S(2)}) copy-start(f32[128]{0:T(128)S(1)} %get-tuple-element.109) | copy-start | bytes 1540
  99.4 148.1 %copy-start = (bf16[1024,1024]{1,0:T(8,128)(2,1)S(1)}, bf16[1024,1024]{1,0:T(8,128)(2,1)}, u32[]{:S(2)}) copy-start(bf16[1024,1024]{1,0:T(8,128)(2,1)} %all-gather.18.cloned.1.call-done) | copy-start | bytes 6291460
  247.5 2.8 copy-start.1
  250.3 90.6 %reduce-scatter.3.cloned.1.call-start = ((), (), s32[]{:S(2)}) async-start(), calls=%async_computation.4 | async-start | bytes 4456448 | tf_op jit(solution)/shard_map/reduce_scatter | solution.py:97
  253.0 0.6 copy-start.5
  253.0 4.8 %copy-start.2 = (f32[2,1,128]{2,1,0:T(1,128)S(1)}, f32[2,1,128]{2,1,0:T(1,128)}, u32[]{:S(2)}) copy-start(f32[2,1,128]{2,1,0:T(1,128)} %all-gather.13) | copy-start | bytes 3076
Sparse Core Ops, SparseCore 0:
  10.1 44.1 all-gather.19
  56.5 40.4 all-gather.17
  250.4 13.1 reduce-scatter.4
  267.8 72.9 reduce-scatter.2
where the time goes:
time: 353 us; the launch traced here: 348 us
  blocking collectives  166 us (47%)
  waiting for transfers between devices  94.5 us (27%)
  local copies, waits for them, and re-layouts  53.7 us (15%)
  between operations  17.5 us (5%)
  matrix products  10.7 us (3%)
  other arithmetic  5.52 us (2%)
    all_gather x10, blocking collectives, joined(): pieces = jax.tree.map(lambda part: lax.all_gather(part, axis), value)  114 us
    dynamic_slice x75, local copies, waits for them, and re-layouts, joined(): lax.scan(lambda subtotal, slab: (join(subtotal, slab), None), head, tail)  46.1 us
    reduce_scatter x1, waiting for transfers between devices, body(): lax.psum_scatter(logit_scale * jnp.dot(picked, text_slab, preferred_eleme...  40.8 us
    psum x1, blocking collectives, body(): loss = lax.psum(partial_value, ('row', 'col')) / pair_count  38.3 us
    all_gather x1, waiting for transfers between devices, body(): lax.all_gather(image_teacher, 'col', axis=0, tiled=True)  31.8 us
    all_gather x1, waiting for transfers between devices, body(): lax.all_gather(image_student, 'col', axis=0, tiled=True)  20.5 us
    all_gather x1, blocking collectives, body(): lax.all_gather(text_student, 'row', axis=0, tiled=True)  7.42 us
  transfers between devices with their start and end apart: 4, of which 3 were waited for; matrix products, arithmetic and copies ran while one was open for 2% of the time, Pallas kernels for 0%

commit v1 on v0

--- a/solution.py
+++ b/solution.py
@@ -4,6 +4,9 @@
 from jax.sharding import PartitionSpec as P
 
 logit_scale = 100.0
+end_spots = lambda vals: jnp.concatenate(
+    lax.all_to_all(jnp.stack([vals] * lax.psum(1, "col")), "col", 0, 0), 0
+)
 
 
 def joined(value, axis, join):
@@ -64,7 +67,7 @@
     per_device = image_student.shape[0]
     image_slab, image_frozen = (
         lax.all_gather(image_student, "col", axis=0, tiled=True),
-        lax.all_gather(image_teacher, "col", axis=0, tiled=True),
+        end_spots(image_teacher),
     )
     text_slab, text_frozen = (
         lax.all_gather(text_student, "row", axis=0, tiled=True),

time: 353 us -> 352 us (level)
  starting transfers between devices: 0.16 us -> 7.64 us
  waiting for transfers between devices: 94.5 us -> 89.6 us
    all_to_all x0 -> x1, waiting for transfers between devices: none -> 32.3 us  [lax.all_to_all(jnp.stack([vals] * lax.psum(1, 'col')), 'col', 0, 0)]
    all_gather x1 -> x0, waiting for transfers between devices: 31.8 us -> none  [body(): lax.all_gather(image_teacher, 'col', axis=0, tiled=True)]
    all_to_all x0 -> x1, starting transfers between devices: none -> 7.52 us  [lax.all_to_all(jnp.stack([vals] * lax.psum(1, 'col')), 'col', 0, 0)]
    all_gather x1, waiting for transfers between devices: 20.5 us -> 15.7 us  [body(): lax.all_gather(image_student, 'col', axis=0, tiled=True)]
  transfers between devices with their start and end apart: 4 -> 4, of which waited for: 3 -> 3; matrix products, arithmetic and copies ran while one was open for 2% -> 1% of each run, Pallas kernels for 0% -> 0%
where the time goes in v1:
time: 352 us; the launch traced here: 347 us
  blocking collectives  164 us (47%)
  waiting for transfers between devices  89.6 us (25%)
  local copies, waits for them, and re-layouts  56.3 us (16%)
  between operations  17.5 us (5%)
  matrix products  8.49 us (2%)
  starting transfers between devices  7.64 us (2%)
  other arithmetic  3.59 us (1%)
    all_gather x10, blocking collectives, joined(): pieces = jax.tree.map(lambda part: lax.all_gather(part, axis), value)  115 us
    dynamic_slice x75, local copies, waits for them, and re-layouts, joined(): lax.scan(lambda subtotal, slab: (join(subtotal, slab), None), head, tail)  46.2 us
    reduce_scatter x1, waiting for transfers between devices, body(): lax.psum_scatter(logit_scale * jnp.dot(picked, text_slab, preferred_eleme...  41 us
    psum x1, blocking collectives, body(): loss = lax.psum(partial_value, ('row', 'col')) / pair_count  36.8 us
    all_to_all x1, waiting for transfers between devices, lax.all_to_all(jnp.stack([vals] * lax.psum(1, 'col')), 'col', 0, 0)  32.3 us
    all_gather x1, waiting for transfers between devices, body(): lax.all_gather(image_student, 'col', axis=0, tiled=True)  15.7 us
    all_to_all x1, starting transfers between devices, lax.all_to_all(jnp.stack([vals] * lax.psum(1, 'col')), 'col', 0, 0)  7.52 us
  transfers between devices with their start and end apart: 4, of which 3 were waited for; matrix products, arithmetic and copies ran while one was open for 1% of the time, Pallas kernels for 0%

profile of v1, /device:TPU:0, one launch (start us, length us, event | category | flops | bytes accessed | tf_op | source)
XLA Modules:
  0.0 347.2 jit_solution(6357916014280418535)
XLA Ops:
  7.2 2.5 stack.2
  9.6 7.5 %all-to-all-start = ((bf16[16,64,1024]{2,1,0:T(8,128)(2,1)}), bf16[16,64,1024]{2,1,0:T(8,128)(2,1)S(1)}, u32[]{:S(2)}, u32[]{:S(2)}) async-start(bf16[16,64,1024]{2,1,0:T(8,128)(2,1)} %stack.2), calls=%async_computation | async-start | bytes 4194304 | tf_op jit(solution)/shard_map/all_to_all | solution.py:8
  18.0 6.5 %all_gather.58 = bf16[128,1024]{1,0:T(8,128)(2,1)S(1)} all-gather(bf16[64,1024]{1,0:T(8,128)(2,1)S(1)} %copy-done.1), channel_id=1, replica_groups=mesh['row'=2,'col'=16] {'row'}, dimensions={0}, use_global_device_ids=true | all-gather | bytes 393216 | tf_op jit(solution)/shard_map/all_gather | solution.py:73
  24.4 5.6 %all_gather.62 = bf16[128,1024]{1,0:T(8,128)(2,1)S(1)} all-gather(bf16[64,1024]{1,0:T(8,128)(2,1)S(1)} %copy-done.2), channel_id=1, replica_groups=mesh['row'=2,'col'=16] {'row'}, dimensions={0}, use_global_device_ids=true | all-gather | bytes 393216 | tf_op jit(solution)/shard_map/all_gather | solution.py:74
  30.1 32.3 %all-to-all-done = bf16[16,64,1024]{2,1,0:T(8,128)(2,1)S(1)} async-done(((bf16[16,64,1024]{2,1,0:T(8,128)(2,1)}), bf16[16,64,1024]{2,1,0:T(8,128)(2,1)S(1)}, u32[]{:S(2)}, u32[]{:S(2)}) %all-to-all-start) | async-done | bytes 2097184 | tf_op jit(solution)/shard_map/all_to_all | solution.py:8
  62.3 0.8 fusion.37
  63.1 15.7 %all-gather.17.cloned.1.call-done = bf16[1024,1024]{1,0:T(8,128)(2,1)} async-done(((bf16[64,1024]{1,0:T(8,128)(2,1)}), bf16[1024,1024]{1,0:T(8,128)(2,1)}) %all-gather.17.cloned.1.call-update) | async-done | bytes 2097168 | tf_op jit(solution)/shard_map/all_gather | solution.py:69
  78.8 2.4 fusion.36
  81.2 1.9 multiply_reduce_fusion
  83.1 19.8 %all-gather.1 = f32[16384]{0:T(1024)S(1)} all-gather(f32[1024]{0:T(1024)S(1)} %get-tuple-element.108), channel_id=3, replica_groups=mesh['row'=2,'col'=16] {'col'}, dimensions={0}, use_global_device_ids=true | all-gather | bytes 69632 | tf_op jit(solution)/shard_map/all_gather | solution.py:13
  102.9 17.6 %all-gather.3 = f32[16384]{0:T(1024)S(1)} all-gather(f32[1024]{0:T(1024)S(1)} %get-tuple-element.104), channel_id=5, replica_groups=mesh['row'=2,'col'=16] {'col'}, dimensions={0}, use_global_device_ids=true | all-gather | bytes 69632 | tf_op jit(solution)/shard_map/all_gather | solution.py:13
  120.5 18.9 %all-gather.4 = f32[16384]{0:T(1024)S(1)} all-gather(f32[1024]{0:T(1024)S(1)} %get-tuple-element.103), channel_id=6, replica_groups=mesh['row'=2,'col'=16] {'col'}, dimensions={0}, use_global_device_ids=true | all-gather | bytes 69632 | tf_op jit(solution)/shard_map/all_gather | solution.py:13
  140.1 17.7 %all-gather = f32[16384]{0:T(1024)S(1)} all-gather(f32[1024]{0:T(1024)S(1)} %get-tuple-element.110), channel_id=2, replica_groups=mesh['row'=2,'col'=16] {'col'}, dimensions={0}, use_global_device_ids=true | all-gather | bytes 69632 | tf_op jit(solution)/shard_map/all_gather | solution.py:13
  158.3 18.8 %all-gather.2 = f32[16384]{0:T(1024)S(1)} all-gather(f32[1024]{0:T(1024)S(1)} %get-tuple-element.112), channel_id=4, replica_groups=mesh['row'=2,'col'=16] {'col'}, dimensions={0}, use_global_device_ids=true | all-gather | bytes 69632 | tf_op jit(solution)/shard_map/all_gather | solution.py:13
  179.1 0.8 reshape.50
  179.9 1.5 reshape.46
  181.4 1.5 reshape.48
  182.9 47.0 %while.2 = (s32[]{:T(128)}, f32[1024]{0:T(1024)S(1)}, f32[1024]{0:T(1024)S(1)}, f32[1024]{0:T(1024)S(1)}, f32[1024]{0:T(1024)S(1)}, /*index=5*/f32[1024]{0:T(102...) while((s32[]{:T(128)}, f32[1024]{0:T(1024)S(1)}, ...), condition=%wide.region_6.7_spmd, body=%wide.region_5.6_spmd.sunk | while | flops 17410 | bytes 123017 | solution.py:16
  183.6 0.8 constant_dynamic-slice_fusion.12
  185.2 0.8 constant_dynamic-slice_fusion.14
  186.0 0.8 constant_dynamic-slice_fusion.11
  186.8 0.8 constant_dynamic-slice_fusion.12
  188.3 0.8 constant_dynamic-slice_fusion.14
  189.1 0.8 constant_dynamic-slice_fusion.11
  189.9 0.8 constant_dynamic-slice_fusion.12
  191.4 0.8 constant_dynamic-slice_fusion.14
  192.3 0.8 constant_dynamic-slice_fusion.11
  193.0 0.8 constant_dynamic-slice_fusion.12
  194.6 0.8 constant_dynamic-slice_fusion.14
  195.4 0.8 constant_dynamic-slice_fusion.11
  196.2 0.8 constant_dynamic-slice_fusion.12
  197.7 0.8 constant_dynamic-slice_fusion.14
  198.5 0.8 constant_dynamic-slice_fusion.11
  199.3 0.8 constant_dynamic-slice_fusion.12
  200.9 0.8 constant_dynamic-slice_fusion.14
  201.7 0.8 constant_dynamic-slice_fusion.11
  202.4 0.8 constant_dynamic-slice_fusion.12
  204.0 0.8 constant_dynamic-slice_fusion.14
  204.8 0.8 constant_dynamic-slice_fusion.11
  205.6 0.8 constant_dynamic-slice_fusion.12
  207.1 0.8 constant_dynamic-slice_fusion.14
  208.7 0.8 constant_dynamic-slice_fusion.12
  210.3 0.8 constant_dynamic-slice_fusion.14
  211.8 0.8 constant_dynamic-slice_fusion.12
  213.4 0.8 constant_dynamic-slice_fusion.14
  215.0 0.8 constant_dynamic-slice_fusion.12
  216.5 0.8 constant_dynamic-slice_fusion.14
  218.1 0.8 constant_dynamic-slice_fusion.12
  219.7 0.8 constant_dynamic-slice_fusion.14
  221.3 0.8 constant_dynamic-slice_fusion.12
  222.8 0.8 constant_dynamic-slice_fusion.14
  224.4 0.8 constant_dynamic-slice_fusion.12
  225.9 0.8 constant_dynamic-slice_fusion.14
  227.5 0.8 constant_dynamic-slice_fusion.12
  229.1 0.8 constant_dynamic-slice_fusion.14
  229.9 4.3 %all-gather.11 = f32[2,1,128]{2,1,0:T(1,128)S(1)} all-gather(f32[1,1,128]{2,1,0:T(1,128)} %bitcast.201), channel_id=8, replica_groups=mesh['row'=2,'col'=16] {'row'}, dimensions={0}, use_global_device_ids=true | all-gather | bytes 1536 | tf_op jit(solution)/shard_map/all_gather | solution.py:13
  234.2 4.4 %all-gather.10 = f32[2,1,128]{2,1,0:T(1,128)S(1)} all-gather(f32[1,1,128]{2,1,0:T(1,128)} %bitcast.198), channel_id=7, replica_groups=mesh['row'=2,'col'=16] {'row'}, dimensions={0}, use_global_device_ids=true | all-gather | bytes 1536 | tf_op jit(solution)/shard_map/all_gather | solution.py:13
  238.6 4.4 %all-gather.14 = f32[2,1,128]{2,1,0:T(1,128)S(1)} all-gather(f32[1,1,128]{2,1,0:T(1,128)} %bitcast.200), channel_id=11, replica_groups=mesh['row'=2,'col'=16] {'row'}, dimensions={0}, use_global_device_ids=true | all-gather | bytes 1536 | tf_op jit(solution)/shard_map/all_gather | solution.py:13
  243.0 4.3 %all-gather.13 = f32[2,1,128]{2,1,0:T(1,128)S(1)} all-gather(f32[1,1,128]{2,1,0:T(1,128)} %bitcast.197), channel_id=10, replica_groups=mesh['row'=2,'col'=16] {'row'}, dimensions={0}, use_global_device_ids=true | all-gather | bytes 1536 | tf_op jit(solution)/shard_map/all_gather | solution.py:13
  247.4 2.6 convolution_multiply_fusion.1
  250.1 2.7 convolution_multiply_fusion
  253.5 4.4 %all-gather.12 = f32[2,1,128]{2,1,0:T(1,128)S(1)} all-gather(f32[1,1,128]{2,1,0:T(1,128)S(1)} %bitcast.199), channel_id=9, replica_groups=mesh['row'=2,'col'=16] {'row'}, dimensions={0}, use_global_device_ids=true | all-gather | bytes 1536 | tf_op jit(solution)/shard_map/all_gather | solution.py:13
  261.0 36.8 %psum.7 = f32[]{:T(128)} all-reduce(f32[]{:T(128)S(6)} %sub.142), channel_id=1, replica_groups=mesh['row'=2,'col'=16] {'row','col'}, use_global_device_ids=true, to_apply=%region_15.16 | all-reduce | flops 1 | bytes 8 | tf_op jit(solution)/shard_map/psum | solution.py:91
  298.5 41.0 %reduce-scatter.3.cloned.1.call-done = f32[64,1024]{1,0:T(8,128)} async-done(((f32[1024,1024]{1,0:T(8,128)}), f32[64,1024]{1,0:T(8,128)}) %reduce-scatter.3.cloned.1.call-update) | async-done | bytes 262160 | tf_op jit(solution)/shard_map/reduce_scatter | solution.py:100
  (126 shorter events, 24.1 us)
Async XLA Ops:
  9.6 8.3 %copy-start.1 = (bf16[64,1024]{1,0:T(8,128)(2,1)S(1)}, bf16[64,1024]{1,0:T(8,128)(2,1)}, u32[]{:S(2)}) copy-start(bf16[64,1024]{1,0:T(8,128)(2,1)} %param.7) | copy-start | bytes 393220
  9.6 14.8 %copy-start.2 = (bf16[64,1024]{1,0:T(8,128)(2,1)S(1)}, bf16[64,1024]{1,0:T(8,128)(2,1)}, u32[]{:S(2)}) copy-start(bf16[64,1024]{1,0:T(8,128)(2,1)} %param.9) | copy-start | bytes 393220
  9.6 52.7 %all-to-all-start = ((bf16[16,64,1024]{2,1,0:T(8,128)(2,1)}), bf16[16,64,1024]{2,1,0:T(8,128)(2,1)S(1)}, u32[]{:S(2)}, u32[]{:S(2)}) async-start(bf16[16,64,1024]{2,1,0:T(8,128)(2,1)} %stack.2), calls=%async_computation | async-start | bytes 4194304 | tf_op jit(solution)/shard_map/all_to_all | solution.py:8
  17.2 61.6 %all-gather.17.cloned.1.call-start = ((), (), s32[]{:S(2)}) async-start(), calls=%async_computation.3 | async-start | bytes 2228224 | tf_op jit(solution)/shard_map/all_gather | solution.py:69
  17.9 280.6 %reduce-scatter.5.cloned.1.call-start = ((), (), s32[]{:S(2)}) async-start(), calls=%async_computation.5 | async-start | bytes 786432 | tf_op jit(solution)/shard_map/reduce_scatter | solution.py:107
  30.1 51.1 %copy-start.3 = (s32[128]{0:T(128)}, s32[128]{0:T(128)S(1)}, u32[]{:S(2)}) copy-start(s32[128]{0:T(128)S(1)} %iota_add_fusion.1) | copy-start | bytes 1540
  63.1 19.9 %copy-start.5 = (f32[128]{0:T(128)}, f32[128]{0:T(128)S(1)}, u32[]{:S(2)}) copy-start(f32[128]{0:T(128)S(1)} %get-tuple-element.111) | copy-start | bytes 1540
  81.2 1.9 copy-start.6
  81.2 166.2 %copy-start = (bf16[1024,1024]{1,0:T(8,128)(2,1)S(1)}, bf16[1024,1024]{1,0:T(8,128)(2,1)}, u32[]{:S(2)}) copy-start(bf16[1024,1024]{1,0:T(8,128)(2,1)} %all-gather.17.cloned.1.call-done) | copy-start | bytes 6291460
  247.4 2.7 copy-start.4
  250.0 89.5 %reduce-scatter.3.cloned.1.call-start = ((), (), s32[]{:S(2)}) async-start(), calls=%async_computation.4 | async-start | bytes 4456448 | tf_op jit(solution)/shard_map/reduce_scatter | solution.py:100
  252.8 0.7 copy-start.7
Sparse Core Ops, SparseCore 0:
  20.1 58.6 all-gather.16
  250.1 11.9 reduce-scatter.4
  266.5 72.9 reduce-scatter.2
